TPU v7x, 32 devices: a whole 2x2x4 slice. The times are simulated.
32 devices in a mesh: sub: 4 (over z), ma: 8 (over y, x, core).
Axes of the slice: x: 2, y: 2, z: 4, core: 2. Of those that a mesh axis runs over, the one named last changes fastest.
Arguments:
- forcing: float32 [2, 256, 2, 64, 512], P(None, 'sub', None, 'ma'), may hold values from -24 to 24
- slot_wavenumber: int32 [64], P('ma'), may hold values from 0 to 511, as said below
- inverse: float32 [4, 2, 64, 64, 512], P('sub'), may hold values from -2 to 2
- edge_weights: float32 [4, 2, 64], P('sub'), may hold values from -1357 to 1357, as said below
Outputs:
- transform_field: float32 [2, 256, 2, 64, 512], P(None, ('sub', 'ma'))
Inputs may be any that keep to these rules, and one draw needn't show every extreme that they name: `slot_wavenumber`: each device's slots hold 4 pairs: slots 2j and 2j + 1 carry a wavenumber m below 256 and 511 - m, in that order; no wavenumber appears twice. `edge_weights`: together with inverse it makes every row of the interface system strictly diagonally dominant with a positive diagonal.
All inputs are finite; a program needn't handle non-finite values.
Results may differ from a plain program's by a relative error of at most 0.0003.
Values sent between devices are 32-bit elements; how exact they have to be, the bound alone decides.
A program may use at most 192 MiB of HBM per device.

v0:
```python
import jax
import jax.numpy as jnp
from jax import lax
from jax.sharding import PartitionSpec as P

HIGH = lax.Precision.HIGHEST


def shifted(shard, axis, by):
    size = lax.axis_size(axis)
    pairs = [(i, i + by) for i in range(size) if 0 <= i + by < size]
    return lax.ppermute(shard, axis, pairs)


def carried_in(value, axis, join, neutral, backward):
    count, mine = (lax.axis_size(axis), lax.axis_index(axis))
    pieces = jax.tree.map(lambda part: lax.all_gather(part, axis), value)
    if backward:
        pieces = jax.tree.map(lambda part: part[::-1], pieces)
        mine = count - 1 - mine
    subtotal = jax.tree.map(
        lambda part, zero: jnp.full_like(part, 0) + jnp.asarray(zero, part.dtype), value, neutral
    )

    def lap(position, subtotal):
        longer = join(subtotal, jax.tree.map(lambda part: part[position], pieces))
        return jax.tree.map(lambda new, old: jnp.where(position < mine, new, old), longer, subtotal)

    return lax.fori_loop(0, count - 1, lap, subtotal)


def widen(values):
    return values[:, None, None, :]


def forward_combine(earlier, later):
    early_block, early_row, early_decay = earlier
    late_block, late_row, late_decay = later
    block = jnp.stack(
        [
            late_block[0] * early_block[0] + late_block[1] * early_block[2],
            late_block[0] * early_block[1] + late_block[1] * early_block[3],
            late_block[2] * early_block[0] + late_block[3] * early_block[2],
            late_block[2] * early_block[1] + late_block[3] * early_block[3],
        ]
    )
    first_row = (
        late_row[0] * widen(early_block[0])
        + late_row[1] * widen(early_block[2])
        + widen(late_decay) * early_row[0]
    )
    second_row = (
        late_row[0] * widen(early_block[1])
        + late_row[1] * widen(early_block[3])
        + widen(late_decay) * early_row[1]
    )
    decay = late_decay * early_decay
    scale = jnp.max(jnp.abs(block), axis=0)
    return (block / scale, jnp.stack([first_row, second_row]) / widen(scale)[None], decay / scale)


def backward_combine(earlier, later):
    early_shift, early_gain = earlier
    late_shift, late_gain = later
    return (late_shift + widen(late_gain) * early_shift, late_gain * early_gain)


def body(forcing, slot_wavenumber, inverse, edge_weights):
    fields, points, halves, slot_count, degrees = forcing.shape
    block_inverse = inverse[0]
    edge_rows = edge_weights[0]
    degree = jnp.arange(degrees, dtype=jnp.int32)
    kept_modes = (degree[None, :] >= slot_wavenumber[:, None]).astype(jnp.float32)
    position = jnp.arange(points, dtype=jnp.int32)
    interior = ((position > 0) & (position < points - 1)).astype(jnp.float32)
    source = forcing * kept_modes[None, None, None, :, :] * interior[None, :, None, None, None]
    particular = jnp.einsum("fpql,fqcml->fpcml", block_inverse, source, precision=HIGH)
    low_slope = jnp.einsum("p,fpcml->fcml", edge_rows[0], particular, precision=HIGH)
    top_slope = jnp.einsum("p,fpcml->fcml", edge_rows[1], particular, precision=HIGH)
    lower_unit = block_inverse[:, :, 0, :]
    upper_unit = block_inverse[:, :, points - 1, :]
    low_influence = jnp.stack(
        [
            jnp.einsum("p,fpl->fl", edge_rows[0], lower_unit, precision=HIGH),
            jnp.einsum("p,fpl->fl", edge_rows[0], upper_unit, precision=HIGH),
        ]
    )
    top_influence = jnp.stack(
        [
            jnp.einsum("p,fpl->fl", edge_rows[1], lower_unit, precision=HIGH),
            jnp.einsum("p,fpl->fl", edge_rows[1], upper_unit, precision=HIGH),
        ]
    )
    sub_index = lax.axis_index("sub")
    owns_interface = sub_index > 0
    has_row = sub_index < lax.axis_size("sub") - 1
    above_slope, above_influence = shifted((low_slope, low_influence), "sub", -1)
    lower_coef = jnp.where(has_row, top_influence[0], 0.0)
    middle_coef = jnp.where(has_row, top_influence[1] - above_influence[0], 1.0)
    upper_coef = jnp.where(has_row, -above_influence[1], 0.0)
    right_side = jnp.where(has_row, above_slope - top_slope, 0.0)
    zero_small = jnp.zeros_like(lower_coef)
    unit_small = jnp.ones_like(lower_coef)
    element = (
        jnp.stack([middle_coef, -lower_coef, upper_coef, zero_small]),
        jnp.stack([right_side, jnp.zeros_like(right_side)]),
        -lower_coef,
    )
    identity = (
        jnp.stack([unit_small, zero_small, zero_small, unit_small]),
        jnp.zeros_like(element[1]),
        unit_small,
    )
    prefix_block, prefix_row, prefix_decay = carried_in(
        element, "sub", forward_combine, identity, False
    )
    theta_now = prefix_block[0]
    ratio_now = prefix_block[2] / theta_now
    reduced = prefix_row[0] / widen(theta_now)
    shift_part = jnp.where(owns_interface, reduced, 0.0)
    gain_part = jnp.where(owns_interface, -ratio_now, 1.0)
    upper_value, upper_gain = carried_in(
        (shift_part, gain_part),
        "sub",
        backward_combine,
        (jnp.zeros_like(shift_part), jnp.ones_like(gain_part)),
        True,
    )
    lower_value = jnp.where(owns_interface, reduced - widen(ratio_now) * upper_value, 0.0)
    relaid = lax.all_to_all(particular, "ma", split_axis=1, concat_axis=3, tiled=True)
    lower_all, upper_all = (
        lax.all_gather(lower_value, "ma", axis=2, tiled=True),
        lax.all_gather(upper_value, "ma", axis=2, tiled=True),
    )
    row_count = relaid.shape[1]
    offset = lax.axis_index("ma") * row_count
    lower_rows = lax.dynamic_slice_in_dim(lower_unit, offset, row_count, 1)
    upper_rows = lax.dynamic_slice_in_dim(upper_unit, offset, row_count, 1)
    relaid = relaid + lower_all[:, None] * lower_rows[:, :, None, None, :]
    return relaid + upper_all[:, None] * upper_rows[:, :, None, None, :]


def solution(mesh):
    return jax.shard_map(
        body,
        mesh=mesh,
        in_specs=(
            P(None, "sub", None, "ma", None),
            P("ma"),
            P("sub", None, None, None, None),
            P("sub", None, None),
        ),
        out_specs=P(None, ("sub", "ma"), None, None, None),
        check_vma=False,
    )
```

profile of v0, /device:TPU:3, one launch (start us, length us, event | category | flops | bytes accessed | tf_op | source)
XLA Modules:
  0.0 232.1 jit_solution(5791358279139209197)
XLA Ops:
  0.0 0.7 fusion.21
  0.7 4.6 %multiply_multiply_fusion = f32[2,64,2,8,512]{4,3,2,1,0:T(8,128)} fusion(f32[2,64,2,8,512]{4,3,2,1,0:T(8,128)} %param.8, f32[64]{0:T(128)S(1)} %and_convert_fusion, f32[8,512]{1,0:T(8,128)S(1)} %fusion.21), kind=kLoop, calls=%fused_computation.30 | loop fusion | flops 2097152 | bytes 8405248 | tf_op jit(solution)/shard_map/mul | solution.py:76
  5.3 8.7 %copy.15 = f32[2,64,2,8,512]{1,3,2,4,0:T(8,128)} copy(f32[2,64,2,8,512]{4,3,2,1,0:T(8,128)} %multiply_multiply_fusion) | data formatting | bytes 8388608 | tf_op jit(solution)/shard_map/mul | solution.py:76
  14.0 30.5 %copy.20 = f32[2,64,64,512,1]{2,1,4,3,0:T(8,128)} copy(f32[2,64,64,512,1]{3,2,1,0,4:T(8,128)} %bitcast.171) | data formatting | bytes 33554432 | tf_op jit(solution)/shard_map/squeeze | solution.py:70
  44.5 57.6 %convolution_bitcast_fusion = f32[2,64,2,8,512]{1,3,2,4,0:T(8,128)} fusion(f32[2,64,2,8,512]{1,3,2,4,0:T(8,128)} %copy.15, f32[2,64,64,512,1]{2,1,4,3,0:T(8,128)} %copy.20), kind=kOutput, calls=%fused_computation.31 | convolution fusion | flops 805306368 | bytes 25165824 | tf_op jit(solution)/shard_map/fpql,fqcml->fpcml/dot_general | solution.py:77
  102.2 7.6 %copy.17 = f32[2,64,2,8,512]{4,3,2,0,1:T(8,128)} copy(f32[2,64,2,8,512]{1,3,2,4,0:T(8,128)} %convolution_bitcast_fusion) | data formatting | bytes 8388608 | tf_op jit(solution)/shard_map/fpql,fqcml->fpcml/transpose | solution.py:77
  109.8 4.7 %all-to-all-start = ((f32[2,64,2,8,512]{4,3,2,0,1:T(8,128)}), f32[2,64,2,8,512]{4,3,2,0,1:T(8,128)}, u32[]{:S(2)}, u32[]{:S(2)}) async-start(f32[2,64,2,8,512]{4,3,2,0,1:T(8,128)} %copy.17), calls=%async_computation | async-start | bytes 8388608 | tf_op jit(solution)/shard_map/all_to_all | solution.py:130
  114.4 2.7 %fusion.42 = (f32[2,64,1,512]{3,2,1,0:T(1,128)S(1)}, f32[2,64,1,512]{3,2,1,0:T(1,128)S(1)}) fusion(f32[2,64,64,512]{3,2,1,0:T(8,128)} %bitcast.172), kind=kLoop, calls=%fused_computation.87 | loop fusion | bytes 1048576 | tf_op jit(solution)/shard_map/slice | solution.py:80
  117.4 0.2 fusion.7
  117.7 1.3 collective-permute-start
  119.0 6.8 %copy.25 = f32[2,64,2,8,512]{4,1,3,2,0:T(8,128)} copy(f32[2,64,2,8,512]{1,3,2,4,0:T(8,128)} %convolution_bitcast_fusion) | data formatting | bytes 8388608 | tf_op jit(solution)/shard_map/fpql,fqcml->fpcml/transpose | solution.py:77
  125.9 4.6 %fusion.30 = f32[1,2,2,8,512]{4,0,3,2,1:T(1,128)S(1)} fusion(f32[2,64,2,8,512]{4,1,3,2,0:T(8,128)} %copy.25, f32[1,2,64]{2,1,0:T(2,128)S(1)} %copy-done.2), kind=kOutput, calls=%fused_computation.73 | convolution fusion | flops 12582912 | bytes 4260352 | tf_op jit(solution)/shard_map/p,fpcml->fcml/dot_general | solution.py:78
  130.5 1.3 collective-permute-start.1
  131.8 0.2 fusion.5
  132.3 2.2 fusion.28
  134.6 12.7 %all-gather.3 = f32[4,2,512]{2,1,0:T(2,128)S(1)} all-gather(f32[1,2,512]{2,1,0:T(2,128)S(1)} %fusion.27), channel_id=4, replica_groups=mesh['sub'=4,'ma'=8] {'sub'}, dimensions={0}, use_global_device_ids=true | all-gather | bytes 20480 | tf_op jit(solution)/shard_map/all_gather | solution.py:17
  147.4 10.2 %all-gather = f32[16,2,512]{2,1,0:T(2,128)S(1)} all-gather(f32[4,2,512]{2,1,0:T(2,128)S(1)} %pad_maximum_fusion.1), channel_id=2, replica_groups=mesh['sub'=4,'ma'=8] {'sub'}, dimensions={0}, use_global_device_ids=true | all-gather | bytes 81920 | tf_op jit(solution)/shard_map/all_gather | solution.py:17
  157.7 13.4 %all-gather.1 = f32[8,2,2,8,512]{4,3,2,1,0:T(8,128)S(1)} all-gather(f32[2,2,2,8,512]{4,3,2,1,0:T(8,128)S(1)} %stack.64), channel_id=3, replica_groups=mesh['sub'=4,'ma'=8] {'sub'}, dimensions={0}, use_global_device_ids=true | all-gather | bytes 655360 | tf_op jit(solution)/shard_map/all_gather | solution.py:17
  171.1 0.7 while.30
  171.8 12.3 %all_gather.35 = f32[4,2,2,8,512]{4,3,2,1,0:T(8,128)S(1)} all-gather(f32[1,2,2,8,512]{4,3,2,1,0:T(8,128)S(1)} %divide_select_fusion.1), channel_id=1, replica_groups=mesh['sub'=4,'ma'=8] {'sub'}, dimensions={0}, use_global_device_ids=true | all-gather | bytes 327680 | tf_op jit(solution)/shard_map/all_gather | solution.py:17
  184.1 10.4 %all_gather.36 = f32[4,2,512]{2,1,0:T(2,128)S(1)} all-gather(f32[1,2,512]{2,1,0:T(2,128)S(1)} %get-tuple-element.309), channel_id=1, replica_groups=mesh['sub'=4,'ma'=8] {'sub'}, dimensions={0}, use_global_device_ids=true | all-gather | bytes 20480 | tf_op jit(solution)/shard_map/all_gather | solution.py:17
  194.7 23.4 %all_gather.38 = f32[2,2,64,512]{3,2,1,0:T(8,128)S(1)} all-gather(f32[2,2,8,512]{3,2,1,0:T(8,128)S(1)} %get-tuple-element.226), channel_id=1, replica_groups=mesh['sub'=4,'ma'=8] {'ma'}, dimensions={2}, use_global_device_ids=true | all-gather | bytes 589824 | tf_op jit(solution)/shard_map/all_gather | solution.py:133
  218.1 8.9 %all_gather.37 = f32[2,2,64,512]{3,2,1,0:T(8,128)S(1)} all-gather(f32[2,2,8,512]{3,2,1,0:T(8,128)S(1)} %fusion.18), channel_id=1, replica_groups=mesh['sub'=4,'ma'=8] {'ma'}, dimensions={2}, use_global_device_ids=true | all-gather | bytes 589824 | tf_op jit(solution)/shard_map/all_gather | solution.py:132
  227.0 5.2 %fusion.4 = f32[2,8,2,64,512]{4,3,2,1,0:T(8,128)} fusion(f32[2,8,2,8,8,512]{5,4,2,0,1,3:T(8,128)} %bitcast.5, f32[2,8,512]{2,1,0:T(8,128)S(1)} %bitcast.175, f32[2,2,64,512]{3,2,1,0:T(8,128)S(1)} %all_gather.38, f32[2,8,512]{2,1,0:T(8,128)S(1)} %bitcast.176, f32[2,2,64,512]{3,2,1,0:T(8,128)S(1)} %all_gather.37), kind=kLoop, calls=%fused_computation.29 | loop fusion | flops 4194304 | bytes 9502720 | tf_op jit(solution)/shard_map/add | solution.py:140
  (62 shorter events, 1.5 us)
Async XLA Ops:
  109.8 7.4 %copy-start.2 = (f32[1,2,64]{2,1,0:T(2,128)S(1)}, f32[1,2,64]{2,1,0:T(2,128)}, u32[]{:S(2)}) copy-start(f32[1,2,64]{2,1,0:T(2,128)} %param.11) | copy-start | bytes 1540
  109.8 117.2 %all-to-all-start = ((f32[2,64,2,8,512]{4,3,2,0,1:T(8,128)}), f32[2,64,2,8,512]{4,3,2,0,1:T(8,128)}, u32[]{:S(2)}, u32[]{:S(2)}) async-start(f32[2,64,2,8,512]{4,3,2,0,1:T(8,128)} %copy.17), calls=%async_computation | async-start | bytes 8388608 | tf_op jit(solution)/shard_map/all_to_all | solution.py:130
  117.7 29.6 %collective-permute-start = (f32[2,2,512]{2,1,0:T(2,128)S(1)}, f32[2,2,512]{2,1,0:T(2,128)S(1)}, u32[]{:S(2)}, u32[]{:S(2)}) collective-permute-start(f32[2,2,512]{2,1,0:T(2,128)S(1)} %pad_maximum_fusion.2), channel_id=1, source_target_pairs={{8,0},{16,8},{24,16},{9,1},{17,9},{25,17},{10,2},{18,10},{26,18},{... | collective-permute-start | bytes 24584 | tf_op jit(solution)/shard_map/ppermute | solution.py:12
  125.9 6.4 %copy-start = (f32[2,64,2,8,512]{4,1,3,2,0:T(8,128)S(1)}, f32[2,64,2,8,512]{4,1,3,2,0:T(8,128)}, u32[]{:S(2)}) copy-start(f32[2,64,2,8,512]{4,1,3,2,0:T(8,128)} %copy.25) | copy-start | bytes 12582916
  130.5 40.6 %copy-start.1 = (f32[4,2,512]{2,1,0:T(2,128)S(1)}, f32[4,2,512]{2,1,0:T(2,128)}, u32[]{:S(2)}) copy-start(f32[4,2,512]{2,1,0:T(2,128)} %constant.74.clone.1) | copy-start | bytes 49156
  130.5 27.1 %collective-permute-start.1 = (f32[2,2,8,512]{3,2,1,0:T(8,128)S(1)}, f32[2,2,8,512]{3,2,1,0:T(8,128)S(1)}, u32[]{:S(2)}, u32[]{:S(2)}) collective-permute-start(f32[2,2,8,512]{3,2,1,0:T(8,128)S(1)} %bitcast.177), channel_id=1, source_target_pairs={{8,0},{16,8},{24,16},{9,1},{17,9},{25,17},{10,2},{18,10},{26,18},{... | collective-permute-start | bytes 196616 | tf_op jit(solution)/shard_map/ppermute | solution.py:12
where the time goes:
time: 235 us; the launch traced here: 232 us
  blocking collectives  91.2 us (39%)
  matrix products  65.5 us (28%)
  local copies, waits for them, and re-layouts  56.5 us (24%)
  other arithmetic  11.2 us (5%)
  starting transfers between devices  7.25 us (3%)
    all_gather x5, blocking collectives, carried_in(): pieces = jax.tree.map(lambda part: lax.all_gather(part, axis), value)  59 us
    dot_general x1, matrix products, body(): jnp.einsum('fpql,fqcml->fpcml', block_inverse, source, precision=HIGH)  57.6 us
    squeeze x1, local copies, waits for them, and re-layouts, body(): block_inverse = inverse[0]  30.5 us
    all_gather x1, blocking collectives, body(): lax.all_gather(upper_value, 'ma', axis=2, tiled=True)  23.4 us
    transpose x2, local copies, waits for them, and re-layouts, body(): jnp.einsum('fpql,fqcml->fpcml', block_inverse, source, precision=HIGH)  14.5 us
    all_gather x1, blocking collectives, body(): lax.all_gather(lower_value, 'ma', axis=2, tiled=True)  8.89 us
    mul x1, local copies, waits for them, and re-layouts, body(): forcing * kept_modes[None, None, None, :, :]  8.66 us
    add x1, other arithmetic, body(): return relaid + upper_all[:, None] * upper_rows[:, :, None, None, :]  5.15 us
  transfers between devices with their start and end apart: 3, of which 0 were waited for; matrix products, arithmetic and copies ran while one was open for 8% of the time, Pallas kernels for 0%

commit v1 on v0

v1 whole, which is shorter than its diff:
```python
import functools

import jax
import jax.numpy as jnp
from jax import lax
from jax.experimental import pallas as pl
from jax.experimental.pallas import tpu as pltpu
from jax.sharding import PartitionSpec as P

LANES = 128
ROWS = 8
F32 = jnp.float32
MESH = pl.DeviceIdType.MESH


def grid_iotas():
    row = lax.broadcasted_iota(jnp.int32, (ROWS, LANES), 0)
    lane = lax.broadcasted_iota(jnp.int32, (ROWS, LANES), 1)
    return row, lane


def lane_gather(values, index):
    return jnp.take_along_axis(values, index, axis=1, mode="promise_in_bounds")


def solve_kernel(
    dims, slot, edge, forcing, inverse, packed, ends, cols, even_src, odd_src, part, edge_sum
):
    fields, points, degrees, group = dims
    tiles = degrees // LANES
    half = tiles // 2
    wide = tiles + half
    blocks = points // ROWS
    g = pl.program_id(0)
    row, lane = grid_iotas()
    is_even = (row & 1) == 0
    m = jnp.zeros((ROWS, LANES), jnp.int32)
    for j in range(ROWS // 2):
        m = jnp.where((row >> 1) == j, slot[2 * j], m)

    @pl.when(g == 0)
    def _():
        ends[...] = jnp.zeros_like(ends)
        edge_sum[...] = jnp.zeros_like(edge_sum)

        def prepare(q, _):
            inside = jnp.where((q > 0) & (q < points - 1), 1.0, 0.0).astype(F32)
            for f in range(fields):
                for t in range(tiles):
                    at = pl.ds(t * LANES, LANES)
                    a = forcing[f, q, 0, :, at] * inside
                    b = forcing[f, q, 1, :, at] * inside
                    degree = lane + t * LANES
                    mixed = jnp.where(is_even, a, pltpu.roll(b, 1, 0))
                    even_src[f, q, t] = jnp.where(degree >= m, mixed, 0.0)
                    if t >= half:
                        mixed = jnp.where(is_even, pltpu.roll(a, ROWS - 1, 0), b)
                        odd_src[f, q, t - half] = jnp.where(degree >= degrees - 1 - m, mixed, 0.0)
            return 0

        lax.fori_loop(0, points, prepare, 0)

    shift_index = (lane - m) & (LANES - 1)
    left_index = (degrees - 1 - m) & (LANES - 1)
    left = jnp.zeros((ROWS, LANES), F32)
    for f in range(fields):
        weights = [[edge[0, e, g * group + p] for p in range(group)] for e in range(2)]
        for t in range(tiles):
            at = pl.ds(t * LANES, LANES)
            both = t >= half

            def step(block, sums, f=f, t=t, at=at, both=both):
                sums = list(sums)
                for i in range(ROWS):
                    q = block * ROWS + i
                    even = even_src[f, q, t]
                    odd = odd_src[f, q, t - half] if both else None
                    for p in range(group):
                        line = inverse[0, f, p, block, pl.ds(i, 1), at]
                        entry = jnp.broadcast_to(line, (ROWS, LANES))
                        sums[p] += entry * even
                        if both:
                            sums[group + p] += entry * odd
                return tuple(sums)

            start = tuple(jnp.zeros((ROWS, LANES), F32) for _ in range(group * (2 if both else 1)))
            sums = lax.fori_loop(0, blocks, step, start)
            for p in range(group):
                part[p, t] = sums[p]
                if both:
                    part[p, tiles + t - half] = sums[group + p]
            for e in range(2):
                base = (e * fields + f) * wide
                ends[base + t] += sum(weights[e][p] * sums[p] for p in range(group))
                if both:
                    ends[base + tiles + t - half] += sum(
                        weights[e][p] * sums[group + p] for p in range(group)
                    )
                for w in range(2):
                    edge_block = w * (blocks - 1)
                    edge_sum[e, f, w, t] += sum(
                        weights[e][p] * inverse[0, f, p, edge_block, :, at] for p in range(group)
                    )
        for p in range(group):
            k = f * group + p
            near, far = part[p, tiles], part[p, tiles + 1]
            near_moved = lane_gather(near, shift_index)
            far_moved = lane_gather(far, shift_index)
            packed[0, k * tiles] = jnp.where(
                lane >= m, part[p, 0], jnp.where(lane - m >= -LANES, far_moved, near_moved)
            )
            packed[0, k * tiles + 1] = jnp.where(lane + LANES >= m, part[p, 1], far_moved)
            packed[0, k * tiles + 2] = part[p, 2]
            packed[0, k * tiles + 3] = part[p, 3]
            spare = jnp.where(
                m < LANES, lane_gather(far, left_index), lane_gather(near, left_index)
            )
            left = jnp.where(lane == k, spare, left)
    packed[0, fields * group * tiles] = left
    packed[0, fields * group * tiles + 1] = m.astype(F32)

    @pl.when(g == lax.axis_index("ma"))
    def _():
        for f in range(fields):
            for p in range(group):
                cols[0, f, pl.ds(p, 1), :] = inverse[0, f, p, 0, pl.ds(0, 1), :]
                cols[1, f, pl.ds(p, 1), :] = inverse[0, f, p, blocks - 1, pl.ds(ROWS - 1, 1), :]

    @pl.when(g == pl.num_programs(0) - 1)
    def _():
        base = 2 * fields * wide
        for f in range(fields):
            for e in range(2):
                for w in range(2):
                    at = f * 4 + e * 2 + w
                    for t in range(wide):
                        source = t if t < tiles else t - half
                        line = edge_sum[e, f, w, source, pl.ds(w * (ROWS - 1), 1), :]
                        ends[base + t, pl.ds(at, 1), :] = line


def exchange_kernel(
    dims, packed, ends, landed, values_landed,
    everyone, values, z_send, z_recv, p_send, p_recv, u_send, u_recv, own_sem,
):
    fields, wide, subs, groups = dims
    sub = lax.axis_index("sub")
    me = lax.axis_index("ma")
    subs_to = [lax.rem(sub + k, subs) for k in range(1, subs)]
    groups_to = [lax.rem(me + k, groups) for k in range(1, groups)]
    barrier = pltpu.get_barrier_semaphore()
    for other in subs_to:
        pl.semaphore_signal(barrier, inc=1, device_id=(other, me), device_id_type=MESH)
    for other in groups_to:
        pl.semaphore_signal(barrier, inc=1, device_id=(sub, other), device_id_type=MESH)
    pl.semaphore_wait(barrier, subs + groups - 2)

    z_copies = []
    for i, other in enumerate(subs_to):
        copy = pltpu.make_async_remote_copy(
            src_ref=ends, dst_ref=everyone.at[sub], send_sem=z_send.at[i], recv_sem=z_recv.at[i],
            device_id=(other, me), device_id_type=MESH,
        )
        copy.start()
        z_copies.append(copy)
    copies = []
    for i, other in enumerate(groups_to):
        copy = pltpu.make_async_remote_copy(
            src_ref=packed.at[other], dst_ref=landed.at[me],
            send_sem=p_send.at[i], recv_sem=p_recv.at[i],
            device_id=(sub, other), device_id_type=MESH,
        )
        copy.start()
        copies.append(copy)
    own = pltpu.make_async_copy(packed.at[me], landed.at[me], own_sem.at[0])
    own.start()
    everyone[sub] = ends[...]
    for copy in z_copies:
        copy.wait()

    base = 2 * fields * wide
    for f in range(fields):
        for t in range(wide):
            def influence(s, e, w):
                line = everyone[s, base + t, pl.ds(f * 4 + e * 2 + w, 1), :]
                return jnp.broadcast_to(line, (ROWS, LANES))

            def slope(s, e):
                return everyone[s, (e * fields + f) * wide + t]

            zero = jnp.zeros((ROWS, LANES), F32)
            ratio, reduced = zero, zero
            ratios, reduceds = [], []
            for k in range(subs - 1):
                low = influence(k, 1, 0)
                middle = influence(k, 1, 1) - influence(k + 1, 0, 0)
                up = -influence(k + 1, 0, 1)
                right = slope(k + 1, 0) - slope(k, 1)
                pivot = middle - low * ratio
                reduced = (right - low * reduced) / pivot
                ratio = up / pivot
                ratios.append(ratio)
                reduceds.append(reduced)
            later = zero
            lower_value, upper_value = zero, zero
            for k in range(subs - 2, -1, -1):
                later = reduceds[k] - ratios[k] * later
                lower_value = jnp.where(sub == k + 1, later, lower_value)
                upper_value = jnp.where(sub == k, later, upper_value)
            values[f * wide + t] = lower_value
            values[(fields + f) * wide + t] = upper_value

    for i, other in enumerate(groups_to):
        copy = pltpu.make_async_remote_copy(
            src_ref=values, dst_ref=values_landed.at[me],
            send_sem=u_send.at[i], recv_sem=u_recv.at[i],
            device_id=(sub, other), device_id_type=MESH,
        )
        copy.start()
        copies.append(copy)
    own_values = pltpu.make_async_copy(values, values_landed.at[me], own_sem.at[1])
    own_values.start()
    own.wait()
    own_values.wait()
    for copy in copies:
        copy.wait()


def finish_kernel(dims, landed, values, cols, out):
    fields, degrees, group = dims
    tiles = degrees // LANES
    half = tiles // 2
    wide = tiles + half
    row, lane = grid_iotas()
    is_even = (row & 1) == 0
    count = fields * group * tiles
    left = landed[0, count]
    m = landed[0, count + 1].astype(jnp.int32)
    back_index = (lane + m) & (LANES - 1)
    for f in range(fields):
        for p in range(group):
            k = f * group + p
            pieces = [landed[0, k * tiles + t] for t in range(tiles)]
            first = lane_gather(pieces[0], back_index)
            second = lane_gather(pieces[1], back_index)
            spare = lane_gather(left, jnp.full((ROWS, LANES), k, jnp.int32))
            even = [
                jnp.where(lane >= m, pieces[0], 0.0),
                jnp.where(lane + LANES >= m, pieces[1], 0.0),
                pieces[2],
                pieces[3],
            ]
            odd = [None] * half
            moved = [first, jnp.where(lane + m < 2 * LANES, first, second)]
            for t in range(half):
                degree = lane + (half + t) * LANES
                odd[t] = jnp.where(
                    degree >= degrees - m,
                    moved[t],
                    jnp.where(degree == degrees - 1 - m, spare, 0.0),
                )
            for t in range(tiles):
                at = pl.ds(t * LANES, LANES)
                low = jnp.broadcast_to(cols[0, f, pl.ds(p, 1), at], (ROWS, LANES))
                top = jnp.broadcast_to(cols[1, f, pl.ds(p, 1), at], (ROWS, LANES))
                e = even[t] + values[0, f * wide + t] * low
                e = e + values[0, (fields + f) * wide + t] * top
                o = jnp.zeros((ROWS, LANES), F32)
                if t >= half:
                    spot = tiles + t - half
                    o = odd[t - half] + values[0, f * wide + spot] * low
                    o = o + values[0, (fields + f) * wide + spot] * top
                out[f, p, 0, :, at] = jnp.where(is_even, e, pltpu.roll(o, 1, 0))
                out[f, p, 1, :, at] = jnp.where(is_even, pltpu.roll(e, ROWS - 1, 0), o)


def body(forcing, slot_wavenumber, inverse, edge_weights):
    fields, points, halves, slots, degrees = forcing.shape
    subs, groups = lax.axis_size("sub"), lax.axis_size("ma")
    group = points // groups
    tiles = degrees // LANES
    half = tiles // 2
    wide = tiles + half
    assert halves == 2 and slots == ROWS and tiles == 4
    count = fields * group * tiles + 2
    end_count = 2 * fields * wide + wide
    value_count = 2 * fields * wide
    shape = jax.ShapeDtypeStruct
    packed, ends, cols = pl.pallas_call(
        functools.partial(solve_kernel, (fields, points, degrees, group)),
        grid=(groups,),
        in_specs=[
            pl.BlockSpec(memory_space=pltpu.SMEM),
            pl.BlockSpec(memory_space=pltpu.SMEM),
            pl.BlockSpec((fields, points, halves, slots, degrees), lambda g: (0, 0, 0, 0, 0)),
            pl.BlockSpec(
                (1, fields, group, points // ROWS, ROWS, degrees), lambda g: (0, 0, g, 0, 0, 0)
            ),
        ],
        out_specs=[
            pl.BlockSpec((1, count, ROWS, LANES), lambda g: (g, 0, 0, 0)),
            pl.BlockSpec((end_count, ROWS, LANES), lambda g: (0, 0, 0)),
            pl.BlockSpec((2, fields, group, degrees), lambda g: (0, 0, 0, 0)),
        ],
        out_shape=[
            shape((groups, count, ROWS, LANES), F32),
            shape((end_count, ROWS, LANES), F32),
            shape((2, fields, group, degrees), F32),
        ],
        scratch_shapes=[
            pltpu.VMEM((fields, points, tiles, ROWS, LANES), F32),
            pltpu.VMEM((fields, points, half, ROWS, LANES), F32),
            pltpu.VMEM((group, wide, ROWS, LANES), F32),
            pltpu.VMEM((2, fields, 2, tiles, ROWS, LANES), F32),
        ],
        compiler_params=pltpu.CompilerParams(vmem_limit_bytes=40 * 1024 * 1024),
    )(
        slot_wavenumber,
        edge_weights,
        forcing,
        inverse.reshape(1, fields, points, points // ROWS, ROWS, degrees),
    )

    landed, values = pl.pallas_call(
        functools.partial(exchange_kernel, (fields, wide, subs, groups)),
        in_specs=[
            pl.BlockSpec(memory_space=pl.ANY),
            pl.BlockSpec(memory_space=pltpu.VMEM),
        ],
        out_specs=[pl.BlockSpec(memory_space=pl.ANY), pl.BlockSpec(memory_space=pl.ANY)],
        out_shape=[
            shape((groups, count, ROWS, LANES), F32),
            shape((groups, value_count, ROWS, LANES), F32),
        ],
        scratch_shapes=[
            pltpu.VMEM((subs, end_count, ROWS, LANES), F32),
            pltpu.VMEM((value_count, ROWS, LANES), F32),
            pltpu.SemaphoreType.DMA((subs - 1,)),
            pltpu.SemaphoreType.DMA((subs - 1,)),
            pltpu.SemaphoreType.DMA((groups - 1,)),
            pltpu.SemaphoreType.DMA((groups - 1,)),
            pltpu.SemaphoreType.DMA((groups - 1,)),
            pltpu.SemaphoreType.DMA((groups - 1,)),
            pltpu.SemaphoreType.DMA((2,)),
        ],
        compiler_params=pltpu.CompilerParams(collective_id=0, has_side_effects=True),
    )(packed, ends)

    return pl.pallas_call(
        functools.partial(finish_kernel, (fields, degrees, group)),
        grid=(groups,),
        in_specs=[
            pl.BlockSpec((1, count, ROWS, LANES), lambda d: (d, 0, 0, 0)),
            pl.BlockSpec((1, value_count, ROWS, LANES), lambda d: (d, 0, 0, 0)),
            pl.BlockSpec((2, fields, group, degrees), lambda d: (0, 0, 0, 0)),
        ],
        out_specs=pl.BlockSpec(
            (fields, group, halves, slots, degrees), lambda d: (0, 0, 0, d, 0)
        ),
        out_shape=shape((fields, group, halves, slots * groups, degrees), F32),
        compiler_params=pltpu.CompilerParams(vmem_limit_bytes=24 * 1024 * 1024),
    )(landed, values, cols)


def solution(mesh):
    return jax.shard_map(
        body,
        mesh=mesh,
        in_specs=(
            P(None, "sub", None, "ma", None),
            P("ma"),
            P("sub", None, None, None, None),
            P("sub", None, None),
        ),
        out_specs=P(None, ("sub", "ma"), None, None, None),
        check_vma=False,
    )
```

time: 235 us -> 74.5 us (0.32)
  blocking collectives: 91.2 us -> 0 us
  matrix products: 65.5 us -> 0 us
  Pallas kernels: 0 us -> 65.1 us
  local copies, waits for them, and re-layouts: 56.5 us -> 8.25 us
  other arithmetic: 11.2 us -> 0 us
  starting transfers between devices: 7.25 us -> 0 us
    all_gather x7 -> x0, blocking collectives: 91.2 us -> none  [the longest x5 59 us: carried_in(): pieces = jax.tree.map(lambda part: lax.all_gather(part, axis), value)]
    dot_general x7 -> x0, matrix products: 65.5 us -> none  [the longest x1 57.6 us: body(): jnp.einsum('fpql,fqcml->fpcml', block_inverse, source, precision=HIGH)]
    pallas_call x0 -> x3, Pallas kernels: none -> 65.1 us  [the longest x1 38.7 us: body(): pl.pallas_call(functools.partial(exchange_kernel, (fields, wide, subs, gr...]
    squeeze x1 -> x0, local copies, waits for them, and re-layouts: 30.5 us -> none  [body(): block_inverse = inverse[0]]
    transpose x2 -> x0, local copies, waits for them, and re-layouts: 14.5 us -> none  [body(): jnp.einsum('fpql,fqcml->fpcml', block_inverse, source, precision=HIGH)]
    mul x7 -> x0, local copies, waits for them, and re-layouts: 8.71 us -> none  [the longest x1 8.66 us: body(): forcing * kept_modes[None, None, None, :, :]]
    unnamed x8 -> x14, local copies, waits for them, and re-layouts: 0.02 us -> 8.25 us
    add x4 -> x0, other arithmetic: 5.28 us -> none  [the longest x1 5.15 us: body(): return relaid + upper_all[:, None] * upper_rows[:, :, None, None, :]]
  transfers between devices with their start and end apart: 3 -> 0, of which waited for: 0 -> 0; matrix products, arithmetic and copies ran while one was open for 8% -> 0% of each run, Pallas kernels for 0% -> 0%
where the time goes in v1:
time: 74.5 us; the launch traced here: 73.4 us
  Pallas kernels  65.1 us (87%)
  local copies, waits for them, and re-layouts  8.25 us (11%)
    pallas_call x1, Pallas kernels, body(): pl.pallas_call(functools.partial(exchange_kernel, (fields, wide, subs, gr...  38.7 us
    pallas_call x1, Pallas kernels, body(): pl.pallas_call(functools.partial(solve_kernel, (fields, points, degrees,...  22.6 us
    unnamed x14, local copies, waits for them, and re-layouts  8.25 us
    pallas_call x1, Pallas kernels, body(): pl.pallas_call(functools.partial(finish_kernel, (fields, degrees, group))...  3.91 us

profile of v1, /device:TPU:3, one launch (start us, length us, event | category | flops | bytes accessed | tf_op | source)
XLA Modules:
  0.0 73.4 jit_solution(13927474872459751641)
XLA Ops:
  0.0 0.0 copy-start
  0.0 2.2 %copy-done = f32[2,64,2,8,512]{4,3,2,1,0:T(8,128)S(1)} copy-done((f32[2,64,2,8,512]{4,3,2,1,0:T(8,128)S(1)}, f32[2,64,2,8,512]{4,3,2,1,0:T(8,128)}, u32[]{:S(2)}) %copy-start) | copy-done | bytes 4194328
  2.2 0.0 copy-start.5
  2.2 0.7 copy-done.5
  2.9 0.0 copy-start.6
  2.9 0.7 copy-done.6
  3.5 22.6 %shard_map.46 = (f32[8,66,8,128]{3,2,1,0:T(8,128)S(1)}, f32[30,8,128]{2,1,0:T(8,128)S(1)}, f32[2,2,8,512]{3,2,1,0:T(8,128)S(1)}) custom-call(s32[8]{0:T(128)S(1)} %copy-done.6, f32[1,2,64]{2,1,0:T(2,128)S(1)} %copy-done.5, f32[2,64,2,8,512]{4,3,2,1,0:T(8,128)S(1)} %copy-done, f32[1,2,64,8,8,512]{5,4,3,2,1,0:T(8,128)} %bitcast.1), custom_call_target="tpu_custom_call" | custom-call | tf_op jit(solution)/shard_map/pallas_call | solution.py:289
  26.1 0.0 copy-start.2
  26.1 1.3 %copy-done.2 = f32[8,66,8,128]{3,2,1,0:T(8,128)} copy-done((f32[8,66,8,128]{3,2,1,0:T(8,128)}, f32[8,66,8,128]{3,2,1,0:T(8,128)S(1)}, u32[]{:S(2)}) %copy-start.2) | copy-done | bytes 2162712
  27.4 0.0 copy-start.4
  27.4 0.7 copy-done.4
  28.1 38.7 %shard_map.47 = (f32[8,66,8,128]{3,2,1,0:T(8,128)}, f32[8,24,8,128]{3,2,1,0:T(8,128)}) custom-call(f32[8,66,8,128]{3,2,1,0:T(8,128)} %copy-done.2, f32[30,8,128]{2,1,0:T(8,128)} %copy-done.4), custom_call_target="tpu_custom_call" | custom-call | tf_op jit(solution)/shard_map/pallas_call | solution.py:324
  66.8 0.0 copy-start.1
  66.8 1.6 %copy-done.1 = f32[8,66,8,128]{3,2,1,0:T(8,128)S(1)} copy-done((f32[8,66,8,128]{3,2,1,0:T(8,128)S(1)}, f32[8,66,8,128]{3,2,1,0:T(8,128)}, u32[]{:S(2)}) %copy-start.1) | copy-done | bytes 2162712
  68.4 0.0 copy-start.3
  68.4 1.1 %copy-done.3 = f32[8,24,8,128]{3,2,1,0:T(8,128)S(1)} copy-done((f32[8,24,8,128]{3,2,1,0:T(8,128)S(1)}, f32[8,24,8,128]{3,2,1,0:T(8,128)}, u32[]{:S(2)}) %copy-start.3) | copy-done | bytes 786456
  69.5 3.9 %shard_map.48 = f32[2,8,2,64,512]{4,3,2,1,0:T(8,128)} custom-call(f32[8,66,8,128]{3,2,1,0:T(8,128)S(1)} %copy-done.1, f32[8,24,8,128]{3,2,1,0:T(8,128)S(1)} %copy-done.3, f32[2,2,8,512]{3,2,1,0:T(8,128)S(1)} %get-tuple-element.14.cols), custom_call_target="tpu_custom_call" | custom-call | tf_op jit(solution)/shard_map/pallas_call | solution.py:349
Async XLA Ops:
  0.0 2.2 %copy-start = (f32[2,64,2,8,512]{4,3,2,1,0:T(8,128)S(1)}, f32[2,64,2,8,512]{4,3,2,1,0:T(8,128)}, u32[]{:S(2)}) copy-start(f32[2,64,2,8,512]{4,3,2,1,0:T(8,128)} %forcing.1) | copy-start | bytes 12582916
  2.2 0.7 copy-start.5
  2.9 0.7 copy-start.6
  26.1 1.3 %copy-start.2 = (f32[8,66,8,128]{3,2,1,0:T(8,128)}, f32[8,66,8,128]{3,2,1,0:T(8,128)S(1)}, u32[]{:S(2)}) copy-start(f32[8,66,8,128]{3,2,1,0:T(8,128)S(1)} %get-tuple-element.10.packed) | copy-start | bytes 6488068
  27.4 0.7 copy-start.4
  66.8 1.6 %copy-start.1 = (f32[8,66,8,128]{3,2,1,0:T(8,128)S(1)}, f32[8,66,8,128]{3,2,1,0:T(8,128)}, u32[]{:S(2)}) copy-start(f32[8,66,8,128]{3,2,1,0:T(8,128)} %get-tuple-element.12.landed) | copy-start | bytes 6488068
  68.4 1.1 %copy-start.3 = (f32[8,24,8,128]{3,2,1,0:T(8,128)S(1)}, f32[8,24,8,128]{3,2,1,0:T(8,128)}, u32[]{:S(2)}) copy-start(f32[8,24,8,128]{3,2,1,0:T(8,128)} %get-tuple-element.13.values) | copy-start | bytes 2359300

commit v2 on v1

v2 whole, which is shorter than its diff:
```python
import functools

import jax
import jax.numpy as jnp
from jax import lax
from jax.experimental import pallas as pl
from jax.experimental.pallas import tpu as pltpu
from jax.sharding import PartitionSpec as P

LANES = 128
ROWS = 8
F32 = jnp.float32
MESH = pl.DeviceIdType.MESH
FIRST = 2
VMEM_BYTES = 60 * 1024 * 1024
EARLY = 2


def grid_iotas():
    row = lax.broadcasted_iota(jnp.int32, (ROWS, LANES), 0)
    lane = lax.broadcasted_iota(jnp.int32, (ROWS, LANES), 1)
    return row, lane


def lane_gather(values, index):
    return jnp.take_along_axis(values, index, axis=1, mode="promise_in_bounds")


def solve_kernel(
    dims, slot, edge, forcing, inverse, landed, values_landed, cols,
    raw, blocks_in, even_src, odd_src, part, weighed, packed, ends, everyone, values,
    raw_sem, in_sem, z_send, z_recv, p_send, p_recv, u_send, u_recv, own_sem,
):
    fields, points, degrees, group, subs, groups = dims
    tiles = degrees // LANES
    half = tiles // 2
    wide = tiles + half
    blocks = points // ROWS
    base = 2 * fields * wide
    sub = lax.axis_index("sub")
    me = lax.axis_index("ma")
    row, lane = grid_iotas()
    is_even = (row & 1) == 0

    def target(i):
        return lax.rem(me + lax.rem(i + FIRST, groups), groups)

    def fetch(i):
        return pltpu.make_async_copy(
            inverse.at[0, :, pl.ds(target(i) * group, group)], blocks_in.at[i], in_sem.at[i]
        )

    def send(i):
        return pltpu.make_async_remote_copy(
            src_ref=packed.at[i], dst_ref=landed.at[me],
            send_sem=p_send.at[i], recv_sem=p_recv.at[i],
            device_id=(sub, target(i)), device_id_type=MESH,
        )

    def send_values(i):
        return pltpu.make_async_remote_copy(
            src_ref=values, dst_ref=values_landed.at[me],
            send_sem=u_send.at[i], recv_sem=u_recv.at[i],
            device_id=(sub, target(i)), device_id_type=MESH,
        )

    others = [i for i in range(groups) if (i + FIRST) % groups != 0]
    mine = groups - FIRST
    load = pltpu.make_async_copy(forcing, raw, raw_sem.at[0])
    load.start()
    for i in range(groups):
        fetch(i).start()
    barrier = pltpu.get_barrier_semaphore()
    subs_to = [lax.rem(sub + k, subs) for k in range(1, subs)]
    for other in subs_to:
        pl.semaphore_signal(barrier, inc=1, device_id=(other, me), device_id_type=MESH)
    for i in others:
        pl.semaphore_signal(barrier, inc=1, device_id=(sub, target(i)), device_id_type=MESH)

    m = jnp.zeros((ROWS, LANES), jnp.int32)
    for j in range(ROWS // 2):
        m = jnp.where((row >> 1) == j, slot[2 * j], m)
    load.wait()

    def prepare(q, _):
        inside = jnp.where((q > 0) & (q < points - 1), 1.0, 0.0).astype(F32)
        for f in range(fields):
            for t in range(tiles):
                at = pl.ds(t * LANES, LANES)
                a = raw[f, q, 0, :, at] * inside
                b = raw[f, q, 1, :, at] * inside
                degree = lane + t * LANES
                mixed = jnp.where(is_even, a, pltpu.roll(b, 1, 0))
                even_src[f, q, t] = jnp.where(degree >= m, mixed, 0.0)
                if t >= half:
                    mixed = jnp.where(is_even, pltpu.roll(a, ROWS - 1, 0), b)
                    odd_src[f, q, t - half] = jnp.where(degree >= degrees - 1 - m, mixed, 0.0)
        return 0

    lax.fori_loop(0, points, prepare, 0)
    pl.semaphore_wait(barrier, subs + groups - 2)

    shift_index = (lane - m) & (LANES - 1)
    left_index = (degrees - 1 - m) & (LANES - 1)

    def solve_group(i):
        left = jnp.zeros((ROWS, LANES), F32)
        for f in range(fields):
            for t in range(tiles):
                at = pl.ds(t * LANES, LANES)
                both = t >= half

                def step(block, sums, f=f, t=t, at=at, both=both):
                    sums = list(sums)
                    for r in range(ROWS):
                        q = block * ROWS + r
                        even = even_src[f, q, t]
                        odd = odd_src[f, q, t - half] if both else None
                        for p in range(group):
                            line = blocks_in[i, f, p, block, pl.ds(r, 1), at]
                            entry = jnp.broadcast_to(line, (ROWS, LANES))
                            sums[p] += entry * even
                            if both:
                                sums[group + p] += entry * odd
                    return tuple(sums)

                count = group * (2 if both else 1)
                start = tuple(jnp.zeros((ROWS, LANES), F32) for _ in range(count))
                sums = lax.fori_loop(0, blocks, step, start)
                for p in range(group):
                    part[p, t] = sums[p]
                    if both:
                        part[p, tiles + t - half] = sums[group + p]
            for p in range(group):
                k = f * group + p
                near, far = part[p, tiles], part[p, tiles + 1]
                near_moved = lane_gather(near, shift_index)
                far_moved = lane_gather(far, shift_index)
                packed[i, k * tiles] = jnp.where(
                    lane >= m, part[p, 0], jnp.where(lane - m >= -LANES, far_moved, near_moved)
                )
                packed[i, k * tiles + 1] = jnp.where(lane + LANES >= m, part[p, 1], far_moved)
                packed[i, k * tiles + 2] = part[p, 2]
                packed[i, k * tiles + 3] = part[p, 3]
                spare = jnp.where(
                    m < LANES, lane_gather(far, left_index), lane_gather(near, left_index)
                )
                left = jnp.where(lane == k, spare, left)
        packed[i, fields * group * tiles] = left
        packed[i, fields * group * tiles + 1] = m.astype(F32)

    own = pltpu.make_async_copy(packed.at[mine], landed.at[me], own_sem.at[0])

    def early(i, _):
        fetch(i).wait()
        solve_group(i)
        send(i).start()
        return 0

    lax.fori_loop(0, EARLY, early, 0)
    for i in range(EARLY, groups):
        fetch(i).wait()

    def weigh(block, _):
        for f in range(fields):
            def add(i, sums, f=f):
                sums = list(sums)
                for p in range(group):
                    low = edge[0, 0, target(i) * group + p]
                    top = edge[0, 1, target(i) * group + p]
                    for t in range(tiles):
                        entry = blocks_in[i, f, p, block, :, pl.ds(t * LANES, LANES)]
                        sums[t] += low * entry
                        sums[tiles + t] += top * entry
                return tuple(sums)

            start = tuple(jnp.zeros((ROWS, LANES), F32) for _ in range(2 * tiles))
            sums = lax.fori_loop(0, groups, add, start)
            for t in range(tiles):
                weighed[0, f, block, t] = sums[t]
                weighed[1, f, block, t] = sums[tiles + t]
        return 0

    lax.fori_loop(0, blocks, weigh, 0)
    for f in range(fields):
        def slope_step(block, sums, f=f):
            sums = list(sums)
            for r in range(ROWS):
                q = block * ROWS + r
                for e in range(2):
                    for t in range(tiles):
                        line = weighed[e, f, block, t, pl.ds(r, 1), :]
                        entry = jnp.broadcast_to(line, (ROWS, LANES))
                        sums[e * wide + t] += entry * even_src[f, q, t]
                        if t >= half:
                            sums[e * wide + t + half] += entry * odd_src[f, q, t - half]
            return tuple(sums)

        start = tuple(jnp.zeros((ROWS, LANES), F32) for _ in range(2 * wide))
        sums = lax.fori_loop(0, blocks, slope_step, start)
        for e in range(2):
            for t in range(wide):
                ends[(e * fields + f) * wide + t] = sums[e * wide + t]
            for w in range(2):
                for t in range(wide):
                    source = t if t < tiles else t - half
                    line = weighed[e, f, w * (blocks - 1), source, pl.ds(w * (ROWS - 1), 1), :]
                    ends[base + t, pl.ds(f * 4 + e * 2 + w, 1), :] = line

    z_copies = []
    for i, other in enumerate(subs_to):
        copy = pltpu.make_async_remote_copy(
            src_ref=ends, dst_ref=everyone.at[sub], send_sem=z_send.at[i], recv_sem=z_recv.at[i],
            device_id=(other, me), device_id_type=MESH,
        )
        copy.start()
        z_copies.append(copy)
    everyone[sub] = ends[...]

    def late(i, _):
        solve_group(i)

        @pl.when(i != mine)
        def _():
            send(i).start()

        @pl.when(i == mine)
        def _():
            own.start()

        return 0

    lax.fori_loop(EARLY, groups, late, 0)
    for f in range(fields):
        for p in range(group):
            cols[0, f, pl.ds(p, 1), :] = blocks_in[mine, f, p, 0, pl.ds(0, 1), :]
            cols[1, f, pl.ds(p, 1), :] = blocks_in[mine, f, p, blocks - 1, pl.ds(ROWS - 1, 1), :]
    for copy in z_copies:
        copy.wait()

    for f in range(fields):
        for t in range(wide):
            def influence(s, e, w):
                line = everyone[s, base + t, pl.ds(f * 4 + e * 2 + w, 1), :]
                return jnp.broadcast_to(line, (ROWS, LANES))

            def slope(s, e):
                return everyone[s, (e * fields + f) * wide + t]

            zero = jnp.zeros((ROWS, LANES), F32)
            ratio, reduced = zero, zero
            ratios, reduceds = [], []
            for k in range(subs - 1):
                low = influence(k, 1, 0)
                middle = influence(k, 1, 1) - influence(k + 1, 0, 0)
                up = -influence(k + 1, 0, 1)
                right = slope(k + 1, 0) - slope(k, 1)
                pivot = middle - low * ratio
                reduced = (right - low * reduced) / pivot
                ratio = up / pivot
                ratios.append(ratio)
                reduceds.append(reduced)
            later = zero
            lower_value, upper_value = zero, zero
            for k in range(subs - 2, -1, -1):
                later = reduceds[k] - ratios[k] * later
                lower_value = jnp.where(sub == k + 1, later, lower_value)
                upper_value = jnp.where(sub == k, later, upper_value)
            values[f * wide + t] = lower_value
            values[(fields + f) * wide + t] = upper_value

    for i in others:
        send_values(i).start()
    own_values = pltpu.make_async_copy(values, values_landed.at[me], own_sem.at[1])
    own_values.start()
    own.wait()
    own_values.wait()
    for i in others:
        send(i).wait()
        send_values(i).wait()


def finish_kernel(dims, landed, values, cols, out):
    fields, degrees, group = dims
    tiles = degrees // LANES
    half = tiles // 2
    wide = tiles + half
    row, lane = grid_iotas()
    is_even = (row & 1) == 0
    count = fields * group * tiles
    left = landed[0, count]
    m = landed[0, count + 1].astype(jnp.int32)
    back_index = (lane + m) & (LANES - 1)
    for f in range(fields):
        for p in range(group):
            k = f * group + p
            pieces = [landed[0, k * tiles + t] for t in range(tiles)]
            first = lane_gather(pieces[0], back_index)
            second = lane_gather(pieces[1], back_index)
            spare = lane_gather(left, jnp.full((ROWS, LANES), k, jnp.int32))
            even = [
                jnp.where(lane >= m, pieces[0], 0.0),
                jnp.where(lane + LANES >= m, pieces[1], 0.0),
                pieces[2],
                pieces[3],
            ]
            odd = [None] * half
            moved = [first, jnp.where(lane + m < 2 * LANES, first, second)]
            for t in range(half):
                degree = lane + (half + t) * LANES
                odd[t] = jnp.where(
                    degree >= degrees - m,
                    moved[t],
                    jnp.where(degree == degrees - 1 - m, spare, 0.0),
                )
            for t in range(tiles):
                at = pl.ds(t * LANES, LANES)
                low = jnp.broadcast_to(cols[0, f, pl.ds(p, 1), at], (ROWS, LANES))
                top = jnp.broadcast_to(cols[1, f, pl.ds(p, 1), at], (ROWS, LANES))
                e = even[t] + values[0, f * wide + t] * low
                e = e + values[0, (fields + f) * wide + t] * top
                o = jnp.zeros((ROWS, LANES), F32)
                if t >= half:
                    spot = tiles + t - half
                    o = odd[t - half] + values[0, f * wide + spot] * low
                    o = o + values[0, (fields + f) * wide + spot] * top
                out[f, p, 0, :, at] = jnp.where(is_even, e, pltpu.roll(o, 1, 0))
                out[f, p, 1, :, at] = jnp.where(is_even, pltpu.roll(e, ROWS - 1, 0), o)


def body(forcing, slot_wavenumber, inverse, edge_weights):
    fields, points, halves, slots, degrees = forcing.shape
    subs, groups = lax.axis_size("sub"), lax.axis_size("ma")
    group = points // groups
    tiles = degrees // LANES
    half = tiles // 2
    wide = tiles + half
    assert halves == 2 and slots == ROWS and tiles == 4
    count = fields * group * tiles + 2
    end_count = 2 * fields * wide + wide
    value_count = 2 * fields * wide
    shape = jax.ShapeDtypeStruct
    blocks = points // ROWS
    landed, values, cols = pl.pallas_call(
        functools.partial(solve_kernel, (fields, points, degrees, group, subs, groups)),
        in_specs=[
            pl.BlockSpec(memory_space=pltpu.SMEM),
            pl.BlockSpec(memory_space=pltpu.SMEM),
            pl.BlockSpec(memory_space=pl.ANY),
            pl.BlockSpec(memory_space=pl.ANY),
        ],
        out_specs=[
            pl.BlockSpec(memory_space=pl.ANY),
            pl.BlockSpec(memory_space=pl.ANY),
            pl.BlockSpec(memory_space=pltpu.VMEM),
        ],
        out_shape=[
            shape((groups, count, ROWS, LANES), F32),
            shape((groups, value_count, ROWS, LANES), F32),
            shape((2, fields, group, degrees), F32),
        ],
        scratch_shapes=[
            pltpu.VMEM((fields, points, halves, slots, degrees), F32),
            pltpu.VMEM((groups, fields, group, blocks, ROWS, degrees), F32),
            pltpu.VMEM((fields, points, tiles, ROWS, LANES), F32),
            pltpu.VMEM((fields, points, half, ROWS, LANES), F32),
            pltpu.VMEM((group, wide, ROWS, LANES), F32),
            pltpu.VMEM((2, fields, blocks, tiles, ROWS, LANES), F32),
            pltpu.VMEM((groups, count, ROWS, LANES), F32),
            pltpu.VMEM((end_count, ROWS, LANES), F32),
            pltpu.VMEM((subs, end_count, ROWS, LANES), F32),
            pltpu.VMEM((value_count, ROWS, LANES), F32),
            pltpu.SemaphoreType.DMA((1,)),
            pltpu.SemaphoreType.DMA((groups,)),
            pltpu.SemaphoreType.DMA((subs - 1,)),
            pltpu.SemaphoreType.DMA((subs - 1,)),
            pltpu.SemaphoreType.DMA((groups,)),
            pltpu.SemaphoreType.DMA((groups,)),
            pltpu.SemaphoreType.DMA((groups,)),
            pltpu.SemaphoreType.DMA((groups,)),
            pltpu.SemaphoreType.DMA((2,)),
        ],
        compiler_params=pltpu.CompilerParams(
            collective_id=0, has_side_effects=True, vmem_limit_bytes=VMEM_BYTES
        ),
    )(
        slot_wavenumber,
        edge_weights,
        forcing,
        inverse.reshape(1, fields, points, blocks, ROWS, degrees),
    )

    return pl.pallas_call(
        functools.partial(finish_kernel, (fields, degrees, group)),
        grid=(groups,),
        in_specs=[
            pl.BlockSpec((1, count, ROWS, LANES), lambda d: (d, 0, 0, 0)),
            pl.BlockSpec((1, value_count, ROWS, LANES), lambda d: (d, 0, 0, 0)),
            pl.BlockSpec((2, fields, group, degrees), lambda d: (0, 0, 0, 0)),
        ],
        out_specs=pl.BlockSpec(
            (fields, group, halves, slots, degrees), lambda d: (0, 0, 0, d, 0)
        ),
        out_shape=shape((fields, group, halves, slots * groups, degrees), F32),
        compiler_params=pltpu.CompilerParams(vmem_limit_bytes=VMEM_BYTES),
    )(landed, values, cols)


def solution(mesh):
    return jax.shard_map(
        body,
        mesh=mesh,
        in_specs=(
            P(None, "sub", None, "ma", None),
            P("ma"),
            P("sub", None, None, None, None),
            P("sub", None, None),
        ),
        out_specs=P(None, ("sub", "ma"), None, None, None),
        check_vma=False,
    )
```

time: 74.5 us -> 58.4 us (0.78); the launches traced: 73.4 us -> 58.1 us
  local copies, waits for them, and re-layouts: 8.25 us -> 0 us
  Pallas kernels: 65.1 us -> 58.1 us
    pallas_call x1 -> x0, Pallas kernels: 38.7 us -> none  [body(): pl.pallas_call(functools.partial(exchange_kernel, (fields, wide, subs, gr...]
    pallas_call x1, Pallas kernels: 22.6 us -> 51.5 us  [body(): pl.pallas_call(functools.partial(solve_kernel, (fields, points, degrees,...]
    unnamed x14 -> x0, local copies, waits for them, and re-layouts: 8.25 us -> none
    pallas_call x1, Pallas kernels: 3.91 us -> 6.63 us  [body(): pl.pallas_call(functools.partial(finish_kernel, (fields, degrees, group))...]
where the time goes in v2:
time: 58.4 us; the launch traced here: 58.1 us
  Pallas kernels  58.1 us (99%)
    pallas_call x1, Pallas kernels, body(): pl.pallas_call(functools.partial(solve_kernel, (fields, points, degrees,...  51.5 us
    pallas_call x1, Pallas kernels, body(): pl.pallas_call(functools.partial(finish_kernel, (fields, degrees, group))...  6.63 us

profile of v2, /device:TPU:3, one launch (start us, length us, event | category | flops | bytes accessed | tf_op | source)
XLA Modules:
  0.0 58.1 jit_solution(12548228568643877783)
XLA Ops:
  0.0 51.5 %shard_map.46 = (f32[8,66,8,128]{3,2,1,0:T(8,128)}, f32[8,24,8,128]{3,2,1,0:T(8,128)}, f32[2,2,8,512]{3,2,1,0:T(8,128)}) custom-call(s32[8]{0:T(128)} %slot.1, f32[1,2,64]{2,1,0:T(2,128)} %edge.1, f32[2,64,2,8,512]{4,3,2,1,0:T(8,128)} %forcing.1, f32[1,2,64,8,8,512]{5,4,3,2,1,0:T(8,128)} %bitcast.1), custom_call_target="tpu_custom_call" | custom-call | tf_op jit(solution)/shard_map/pallas_call | solution.py:344
  51.5 6.6 %shard_map.47 = f32[2,8,2,64,512]{4,3,2,1,0:T(8,128)} custom-call(f32[8,66,8,128]{3,2,1,0:T(8,128)} %get-tuple-element.8.landed, f32[8,24,8,128]{3,2,1,0:T(8,128)} %get-tuple-element.9.values, f32[2,2,8,512]{3,2,1,0:T(8,128)} %get-tuple-element.10.cols), custom_call_target="tpu_custom_call" | custom-call | tf_op jit(solution)/shard_map/pallas_call | solution.py:393

commit v3 on v2

--- a/solution.py
+++ b/solution.py
@@ -29,7 +29,7 @@
 def solve_kernel(
     dims, slot, edge, forcing, inverse, landed, values_landed, cols,
     raw, blocks_in, even_src, odd_src, part, weighed, packed, ends, everyone, values,
-    raw_sem, in_sem, z_send, z_recv, p_send, p_recv, u_send, u_recv, own_sem,
+    raw_sem, in_sem, z_send, z_recv, p_send, p_recv, u_send, u_recv, f_send, f_recv, own_sem,
 ):
     fields, points, degrees, group, subs, groups = dims
     tiles = degrees // LANES
@@ -57,19 +57,30 @@
             device_id=(sub, target(i)), device_id_type=MESH,
         )
 
-    def send_values(i):
+    pair = me + 1 - 2 * lax.rem(me, 2)
+    senders = [lax.rem(me + groups - k, groups) for k in range(0, groups, 2)]
+
+    def send_values(k):
+        to = pair if k == 0 else lax.rem(me + k, groups)
         return pltpu.make_async_remote_copy(
             src_ref=values, dst_ref=values_landed.at[me],
-            send_sem=u_send.at[i], recv_sem=u_recv.at[i],
-            device_id=(sub, target(i)), device_id_type=MESH,
+            send_sem=u_send.at[k // 2], recv_sem=u_recv.at[k // 2],
+            device_id=(sub, to), device_id_type=MESH,
+        )
+
+    def forward(k):
+        block = values_landed.at[senders[k // 2]]
+        return pltpu.make_async_remote_copy(
+            src_ref=block, dst_ref=block,
+            send_sem=f_send.at[k // 2], recv_sem=f_recv.at[k // 2],
+            device_id=(sub, pair), device_id_type=MESH,
         )
 
     others = [i for i in range(groups) if (i + FIRST) % groups != 0]
     mine = groups - FIRST
     load = pltpu.make_async_copy(forcing, raw, raw_sem.at[0])
     load.start()
-    for i in range(groups):
-        fetch(i).start()
+    fetch(0).start()
     barrier = pltpu.get_barrier_semaphore()
     subs_to = [lax.rem(sub + k, subs) for k in range(1, subs)]
     for other in subs_to:
@@ -81,6 +92,8 @@
     for j in range(ROWS // 2):
         m = jnp.where((row >> 1) == j, slot[2 * j], m)
     load.wait()
+    for i in range(1, groups):
+        fetch(i).start()
 
     def prepare(q, _):
         inside = jnp.where((q > 0) & (q < points - 1), 1.0, 0.0).astype(F32)
@@ -269,63 +282,95 @@
             values[f * wide + t] = lower_value
             values[(fields + f) * wide + t] = upper_value
 
-    for i in others:
-        send_values(i).start()
+    for k in list(range(2, groups, 2)) + [0]:
+        send_values(k).start()
     own_values = pltpu.make_async_copy(values, values_landed.at[me], own_sem.at[1])
     own_values.start()
+    for k in range(2, groups, 2):
+        send_values(k).wait_recv()
+        forward(k).start()
     own.wait()
     own_values.wait()
     for i in others:
         send(i).wait()
-        send_values(i).wait()
-
-
-def finish_kernel(dims, landed, values, cols, out):
-    fields, degrees, group = dims
+    send_values(0).wait()
+    for k in range(2, groups, 2):
+        send_values(k).wait_send()
+        forward(k).wait()
+
+
+def finish_kernel(
+    dims, landed_in, values_in, cols, result, landed, values, out, landed_sem, values_sem, out_sem
+):
+    fields, degrees, group, groups = dims
     tiles = degrees // LANES
     half = tiles // 2
     wide = tiles + half
+
+    def take(d):
+        return pltpu.make_async_copy(landed_in.at[d], landed.at[d], landed_sem.at[d])
+
+    def take_values(d):
+        return pltpu.make_async_copy(values_in.at[d], values.at[d], values_sem.at[d])
+
+    def put(d):
+        rows = pl.ds(pl.multiple_of(d * ROWS, ROWS), ROWS)
+        return pltpu.make_async_copy(out.at[d], result.at[:, :, :, rows, :], out_sem.at[d])
+
+    for d in range(groups):
+        take(d).start()
+        take_values(d).start()
     row, lane = grid_iotas()
     is_even = (row & 1) == 0
-    count = fields * group * tiles
-    left = landed[0, count]
-    m = landed[0, count + 1].astype(jnp.int32)
-    back_index = (lane + m) & (LANES - 1)
-    for f in range(fields):
-        for p in range(group):
-            k = f * group + p
-            pieces = [landed[0, k * tiles + t] for t in range(tiles)]
-            first = lane_gather(pieces[0], back_index)
-            second = lane_gather(pieces[1], back_index)
-            spare = lane_gather(left, jnp.full((ROWS, LANES), k, jnp.int32))
-            even = [
-                jnp.where(lane >= m, pieces[0], 0.0),
-                jnp.where(lane + LANES >= m, pieces[1], 0.0),
-                pieces[2],
-                pieces[3],
-            ]
-            odd = [None] * half
-            moved = [first, jnp.where(lane + m < 2 * LANES, first, second)]
-            for t in range(half):
-                degree = lane + (half + t) * LANES
-                odd[t] = jnp.where(
-                    degree >= degrees - m,
-                    moved[t],
-                    jnp.where(degree == degrees - 1 - m, spare, 0.0),
-                )
-            for t in range(tiles):
-                at = pl.ds(t * LANES, LANES)
-                low = jnp.broadcast_to(cols[0, f, pl.ds(p, 1), at], (ROWS, LANES))
-                top = jnp.broadcast_to(cols[1, f, pl.ds(p, 1), at], (ROWS, LANES))
-                e = even[t] + values[0, f * wide + t] * low
-                e = e + values[0, (fields + f) * wide + t] * top
-                o = jnp.zeros((ROWS, LANES), F32)
-                if t >= half:
-                    spot = tiles + t - half
-                    o = odd[t - half] + values[0, f * wide + spot] * low
-                    o = o + values[0, (fields + f) * wide + spot] * top
-                out[f, p, 0, :, at] = jnp.where(is_even, e, pltpu.roll(o, 1, 0))
-                out[f, p, 1, :, at] = jnp.where(is_even, pltpu.roll(e, ROWS - 1, 0), o)
+
+    def unpack(d, _):
+        take(d).wait()
+        take_values(d).wait()
+        count = fields * group * tiles
+        left = landed[d, count]
+        m = landed[d, count + 1].astype(jnp.int32)
+        back_index = (lane + m) & (LANES - 1)
+        for f in range(fields):
+            for p in range(group):
+                k = f * group + p
+                pieces = [landed[d, k * tiles + t] for t in range(tiles)]
+                first = lane_gather(pieces[0], back_index)
+                second = lane_gather(pieces[1], back_index)
+                spare = lane_gather(left, jnp.full((ROWS, LANES), k, jnp.int32))
+                even = [
+                    jnp.where(lane >= m, pieces[0], 0.0),
+                    jnp.where(lane + LANES >= m, pieces[1], 0.0),
+                    pieces[2],
+                    pieces[3],
+                ]
+                odd = [None] * half
+                moved = [first, jnp.where(lane + m < 2 * LANES, first, second)]
+                for t in range(half):
+                    degree = lane + (half + t) * LANES
+                    odd[t] = jnp.where(
+                        degree >= degrees - m,
+                        moved[t],
+                        jnp.where(degree == degrees - 1 - m, spare, 0.0),
+                    )
+                for t in range(tiles):
+                    at = pl.ds(t * LANES, LANES)
+                    low = jnp.broadcast_to(cols[0, f, pl.ds(p, 1), at], (ROWS, LANES))
+                    top = jnp.broadcast_to(cols[1, f, pl.ds(p, 1), at], (ROWS, LANES))
+                    e = even[t] + values[d, f * wide + t] * low
+                    e = e + values[d, (fields + f) * wide + t] * top
+                    o = jnp.zeros((ROWS, LANES), F32)
+                    if t >= half:
+                        spot = tiles + t - half
+                        o = odd[t - half] + values[d, f * wide + spot] * low
+                        o = o + values[d, (fields + f) * wide + spot] * top
+                    out[d, f, p, 0, :, at] = jnp.where(is_even, e, pltpu.roll(o, 1, 0))
+                    out[d, f, p, 1, :, at] = jnp.where(is_even, pltpu.roll(e, ROWS - 1, 0), o)
+        put(d).start()
+        return 0
+
+    lax.fori_loop(0, groups, unpack, 0)
+    for d in range(groups):
+        put(d).wait()
 
 
 def body(forcing, slot_wavenumber, inverse, edge_weights):
@@ -376,8 +421,10 @@
             pltpu.SemaphoreType.DMA((subs - 1,)),
             pltpu.SemaphoreType.DMA((groups,)),
             pltpu.SemaphoreType.DMA((groups,)),
-            pltpu.SemaphoreType.DMA((groups,)),
-            pltpu.SemaphoreType.DMA((groups,)),
+            pltpu.SemaphoreType.DMA((groups // 2,)),
+            pltpu.SemaphoreType.DMA((groups // 2,)),
+            pltpu.SemaphoreType.DMA((groups // 2,)),
+            pltpu.SemaphoreType.DMA((groups // 2,)),
             pltpu.SemaphoreType.DMA((2,)),
         ],
         compiler_params=pltpu.CompilerParams(
@@ -391,17 +438,22 @@
     )
 
     return pl.pallas_call(
-        functools.partial(finish_kernel, (fields, degrees, group)),
-        grid=(groups,),
+        functools.partial(finish_kernel, (fields, degrees, group, groups)),
         in_specs=[
-            pl.BlockSpec((1, count, ROWS, LANES), lambda d: (d, 0, 0, 0)),
-            pl.BlockSpec((1, value_count, ROWS, LANES), lambda d: (d, 0, 0, 0)),
-            pl.BlockSpec((2, fields, group, degrees), lambda d: (0, 0, 0, 0)),
-        ],
-        out_specs=pl.BlockSpec(
-            (fields, group, halves, slots, degrees), lambda d: (0, 0, 0, d, 0)
-        ),
+            pl.BlockSpec(memory_space=pl.ANY),
+            pl.BlockSpec(memory_space=pl.ANY),
+            pl.BlockSpec(memory_space=pltpu.VMEM),
+        ],
+        out_specs=pl.BlockSpec(memory_space=pl.ANY),
         out_shape=shape((fields, group, halves, slots * groups, degrees), F32),
+        scratch_shapes=[
+            pltpu.VMEM((groups, count, ROWS, LANES), F32),
+            pltpu.VMEM((groups, value_count, ROWS, LANES), F32),
+            pltpu.VMEM((groups, fields, group, halves, slots, degrees), F32),
+            pltpu.SemaphoreType.DMA((groups,)),
+            pltpu.SemaphoreType.DMA((groups,)),
+            pltpu.SemaphoreType.DMA((groups,)),
+        ],
         compiler_params=pltpu.CompilerParams(vmem_limit_bytes=VMEM_BYTES),
     )(landed, values, cols)
 

time: 58.4 us -> 49.7 us (0.85)
  Pallas kernels: 58.1 us -> 49.4 us
    pallas_call x1, Pallas kernels: 51.5 us -> 45.3 us  [body(): pl.pallas_call(functools.partial(solve_kernel, (fields, points, degrees,...]
    pallas_call x1, Pallas kernels: 6.63 us -> 4.16 us  [body(): pl.pallas_call(functools.partial(finish_kernel, (fields, degrees, group,...]
where the time goes in v3:
time: 49.7 us; the launch traced here: 49.5 us
  Pallas kernels  49.4 us (99%)
    pallas_call x1, Pallas kernels, body(): pl.pallas_call(functools.partial(solve_kernel, (fields, points, degrees,...  45.3 us
    pallas_call x1, Pallas kernels, body(): pl.pallas_call(functools.partial(finish_kernel, (fields, degrees, group,...  4.16 us

profile of v3, /device:TPU:3, one launch (start us, length us, event | category | flops | bytes accessed | tf_op | source)
XLA Modules:
  0.0 49.5 jit_solution(4856688220800435425)
XLA Ops:
  0.0 45.3 %shard_map.46 = (f32[8,66,8,128]{3,2,1,0:T(8,128)}, f32[8,24,8,128]{3,2,1,0:T(8,128)}, f32[2,2,8,512]{3,2,1,0:T(8,128)}) custom-call(s32[8]{0:T(128)} %slot.1, f32[1,2,64]{2,1,0:T(2,128)} %edge.1, f32[2,64,2,8,512]{4,3,2,1,0:T(8,128)} %forcing.1, f32[1,2,64,8,8,512]{5,4,3,2,1,0:T(8,128)} %bitcast.1), custom_call_target="tpu_custom_call" | custom-call | tf_op jit(solution)/shard_map/pallas_call | solution.py:389
  45.3 4.2 %shard_map.47 = f32[2,8,2,64,512]{4,3,2,1,0:T(8,128)} custom-call(f32[8,66,8,128]{3,2,1,0:T(8,128)} %get-tuple-element.8.landed_in, f32[8,24,8,128]{3,2,1,0:T(8,128)} %get-tuple-element.9.values_in, f32[2,2,8,512]{3,2,1,0:T(8,128)} %get-tuple-element.10.cols), custom_call_target="tpu_custom_call" | custom-call | tf_op jit(solution)/shard_map/pallas_call | solution.py:440
